TPU v7x, 32 devices: a whole 2x2x4 slice. The times are simulated.
32 devices in a mesh: hid: 2 (over x), wide: 16 (over z, y, core).
Axes of the slice: x: 2, y: 2, z: 4, core: 2. Of those that a mesh axis runs over, the one named last changes fastest.
Arguments:
- token_ids: int32 [2, 32, 128], P(None, 'hid'), may hold values from 0 to 152063, as said below
- segment_ids: int32 [2, 32, 128], P(None, ('hid', 'wide')), may hold values from 0 to 3, never falling along the last dimension, each value on 1 to 64 neighbouring positions
- step_ends: int32 [2, 32, 4], P(None, ('hid', 'wide')), may hold values from 0 to 127
- step_labels: int32 [2, 32, 4], P(None, 'hid'), may hold values from -1 to 2
- step_count: int32 [], replicated, may hold values from 2 to 20
- table: float32 [152064, 896], P(('hid', 'wide')), may hold values from -0.375 to 0.375
- attn_in: float32 [896, 1152], P('wide', 'hid'), may hold values from -0.1875 to 0.1875
- attn_out: float32 [896, 896], P('wide', 'hid'), may hold values from -0.078125 to 0.078125
- mlp_in: float32 [896, 2, 4864], P('wide', None, 'hid'), may hold values from -0.1875 to 0.1875
- mlp_out: float32 [4864, 896], P('hid', 'wide'), may hold values from -0.015625 to 0.015625
- small_params: float32 [3840], P(('hid', 'wide')), may hold values from -0.5 to 1.5
- table_first: float32 [152064, 896], P(('hid', 'wide')), may hold values from -1.1920929e-06 to 1.1920929e-06
- attn_in_first: float32 [896, 1152], P('wide', 'hid'), may hold values from -1.5258789e-05 to 1.5258789e-05
- attn_out_first: float32 [896, 896], P('wide', 'hid'), may hold values from -1.5258789e-05 to 1.5258789e-05
- mlp_in_first: float32 [896, 2, 4864], P('wide', None, 'hid'), may hold values from -4.7683716e-06 to 4.7683716e-06
- mlp_out_first: float32 [4864, 896], P('hid', 'wide'), may hold values from -7.6293945e-06 to 7.6293945e-06
- small_first: float32 [3840], P(('hid', 'wide')), may hold values from -0.00024414062 to 0.00024414062
- table_second: float32 [152064, 896], P(('hid', 'wide')), may hold values from 1.908266e-13 to 7.779854e-13
- attn_in_second: float32 [896, 1152], P('wide', 'hid'), may hold values from 2.5189113e-11 to 1.02694075e-10
- attn_out_second: float32 [896, 896], P('wide', 'hid'), may hold values from 3.2386e-11 to 1.3203523e-10
- mlp_in_second: float32 [896, 2, 4864], P('wide', None, 'hid'), may hold values from 2.9829212e-12 to 1.216114e-11
- mlp_out_second: float32 [4864, 896], P('hid', 'wide'), may hold values from 5.9658424e-12 to 2.432228e-11
- small_second: float32 [3840], P(('hid', 'wide')), may hold values from 6.7708332e-09 to 2.7604166e-08
Outputs:
- loss: float32 [], replicated
- grad_norm: float32 [], replicated
- table_new: float32 [152064, 896], P(('hid', 'wide'))
- table_first_new: float32 [152064, 896], P(('hid', 'wide'))
- table_second_new: float32 [152064, 896], P(('hid', 'wide'))
- attn_in_new: float32 [896, 1152], P('wide', 'hid')
- attn_in_first_new: float32 [896, 1152], P('wide', 'hid')
- attn_in_second_new: float32 [896, 1152], P('wide', 'hid')
- attn_out_new: float32 [896, 896], P('wide', 'hid')
- attn_out_first_new: float32 [896, 896], P('wide', 'hid')
- attn_out_second_new: float32 [896, 896], P('wide', 'hid')
- mlp_in_new: float32 [896, 2, 4864], P('wide', None, 'hid')
- mlp_in_first_new: float32 [896, 2, 4864], P('wide', None, 'hid')
- mlp_in_second_new: float32 [896, 2, 4864], P('wide', None, 'hid')
- mlp_out_new: float32 [4864, 896], P('hid', 'wide')
- mlp_out_first_new: float32 [4864, 896], P('hid', 'wide')
- mlp_out_second_new: float32 [4864, 896], P('hid', 'wide')
- small_new: float32 [3840], P(('hid', 'wide'))
- small_first_new: float32 [3840], P(('hid', 'wide'))
- small_second_new: float32 [3840], P(('hid', 'wide'))
Inputs may be any that keep to these rules, and one draw needn't show every extreme that they name: `token_ids`: call id // 4752 the block of an id; in every sequence at most 16 tokens have blocks with the same remainder modulo 16, and in every sequence some remainder has exactly 16 of them.
All inputs are finite; a program needn't handle non-finite values.
Results may differ from a plain program's by a relative error of at most 0.02.
Values may be sent and summed in bfloat16 or wider, within the bound.
A program may use at most 224 MiB of HBM per device.

v0:
```python
import jax
import jax.numpy as jnp
from jax import lax
from jax.sharding import PartitionSpec as P

D = 896
HEADS = 14
KV_HEADS = 2
HEAD = 64
ATT = 896
GROUP = 7


norm_eps = 1e-06
rope_base = 1000000.0
plus_token = 10
minus_token = 12
clip_limit = 0.05
beta_one = 0.9
beta_two = 0.95
adam_eps = 1e-08
decay_rate = 0.1
rates = (0.03, 0.015, 0.015, 0.015, 0.0015, 0.3)


def combined_all(array, axis, combine):
    everything = jax.tree.map(lambda part: lax.all_gather(part, axis), array)
    initial = jax.tree.map(lambda part: part[0], everything)

    def turn(k, so_far):
        return combine(so_far, jax.tree.map(lambda part: part[k], everything))

    return lax.fori_loop(1, lax.axis_size(axis), turn, initial)


def rms_scale(rows, gain):
    return rows * lax.rsqrt(jnp.mean(rows * rows, axis=-1, keepdims=True) + norm_eps) * gain


def positions_of(segment):
    places = jnp.arange(segment.shape[0], dtype=jnp.int32)
    starts = jnp.concatenate([jnp.ones((1,), dtype=bool), segment[1:] != segment[:-1]])
    opening = lax.cummax(jnp.where(starts, places, 0), axis=0)
    return (places - opening).astype(jnp.float32)


def angles_of(positions):
    half_size = HEAD // 2
    frequency = rope_base ** (-jnp.arange(half_size, dtype=jnp.float32) / half_size)
    return positions[:, None] * frequency[None, :]


def rotate(values, angles, sign):
    half_size = values.shape[-1] // 2
    cosine = jnp.cos(angles)[:, None, :]
    sine_part = sign * jnp.sin(angles)[:, None, :]
    leading = values[..., :half_size]
    trailing = values[..., half_size:]
    return jnp.concatenate(
        [leading * cosine - trailing * sine_part, trailing * cosine + leading * sine_part], axis=-1
    )


def causal_mask(segment):
    places = jnp.arange(segment.shape[0])
    return (segment[:, None] == segment[None, :]) & (places[:, None] >= places[None, :])


def masked_scores(queries, keys, allowed):
    product = jnp.einsum("skgd,tkd->kgst", queries, keys, preferred_element_type=jnp.float32)
    return jnp.where(allowed[None, None], product * HEAD ** (-0.5), -1e30)


def combine_stats(earlier, later):
    top = jnp.maximum(earlier[0], later[0])
    total = earlier[1] * jnp.exp(earlier[0] - top) + later[1] * jnp.exp(later[0] - top)
    return (top, total, earlier[2] + later[2], earlier[3] + later[3])


def add_tuples(left, right):
    if left is None:
        return right
    return jax.tree.map(jnp.add, left, right)


def local_rows(ids, block_rows, wide_count, limit):
    return jnp.clip(ids // block_rows // wide_count * block_rows + ids % block_rows, 0, limit - 1)


def per_device(
    token_ids,
    segment_ids,
    step_ends,
    step_labels,
    step_count,
    table,
    attn_in,
    attn_out,
    mlp_in,
    mlp_out,
    small_params,
    table_first,
    attn_in_first,
    attn_out_first,
    mlp_in_first,
    mlp_out_first,
    small_first,
    table_second,
    attn_in_second,
    attn_out_second,
    mlp_in_second,
    mlp_out_second,
    small_second,
):
    wide_index = lax.axis_index("wide")
    wide_count = lax.axis_size("wide")
    hid_count = lax.axis_size("hid")
    micro_count = segment_ids.shape[0]
    seq_len = segment_ids.shape[2]
    slots = step_ends.shape[2]
    block_rows = table.shape[0]
    gathered_rows = hid_count * block_rows
    ff_local = mlp_in.shape[2]
    row_iota = jnp.arange(gathered_rows, dtype=jnp.int32)
    global_of = (
        row_iota // block_rows * wide_count + wide_index
    ) * block_rows + row_iota % block_rows
    weights = None
    pending = None
    totals = None
    loss_local = jnp.zeros((), jnp.float32)
    count_local = jnp.zeros((), jnp.float32)
    for micro_batch in range(micro_count):
        weights = (
            lax.all_gather(table.astype(jnp.bfloat16), "hid", axis=0, tiled=True),
            lax.all_gather(
                lax.all_gather(attn_in.astype(jnp.bfloat16), "wide", axis=0, tiled=True),
                "hid",
                axis=1,
                tiled=True,
            ),
            lax.all_gather(
                lax.all_gather(attn_out.astype(jnp.bfloat16), "wide", axis=0, tiled=True),
                "hid",
                axis=1,
                tiled=True,
            ),
            lax.all_gather(mlp_in.astype(jnp.bfloat16), "wide", axis=0, tiled=True).reshape(
                D, 2 * ff_local
            ),
            lax.all_gather(mlp_out.astype(jnp.bfloat16), "wide", axis=1, tiled=True),
            lax.all_gather(
                lax.all_gather(small_params.astype(jnp.bfloat16), "wide", axis=0, tiled=True),
                "hid",
                axis=0,
                tiled=True,
            ),
        )
        table_low, weight_in, weight_out, gate_up, weight_down, smalls = weights
        gains = smalls[: 3 * D].astype(jnp.float32).reshape(3, D)
        bias = smalls[3 * D :].astype(jnp.float32)
        id_rows = token_ids[micro_batch]
        group_ids = id_rows.reshape(-1)
        inside = group_ids // block_rows % wide_count == wide_index
        safe_ids = local_rows(group_ids, block_rows, wide_count, gathered_rows)
        picked = jnp.where(inside[:, None], table_low[safe_ids], jnp.zeros((), jnp.bfloat16))
        embedded = lax.psum_scatter(picked, "wide", scatter_dimension=0, tiled=True).astype(
            jnp.float32
        )
        segment = segment_ids[micro_batch, 0]
        angles = angles_of(positions_of(segment))
        allowed = causal_mask(segment)
        normed_one = rms_scale(embedded, gains[0]).astype(jnp.bfloat16)
        linear = jnp.dot(normed_one, weight_in, preferred_element_type=jnp.float32) + bias
        queries = (
            rotate(linear[:, :ATT].reshape(seq_len, HEADS, HEAD), angles, 1.0)
            .astype(jnp.bfloat16)
            .reshape(seq_len, KV_HEADS, GROUP, HEAD)
        )
        keys = rotate(
            linear[:, ATT : ATT + KV_HEADS * HEAD].reshape(seq_len, KV_HEADS, HEAD), angles, 1.0
        ).astype(jnp.bfloat16)
        values = (
            linear[:, ATT + KV_HEADS * HEAD :].reshape(seq_len, KV_HEADS, HEAD).astype(jnp.bfloat16)
        )
        scores = masked_scores(queries, keys, allowed)
        log_totals = jax.nn.logsumexp(scores, axis=-1, keepdims=True)
        probs = jnp.exp(scores - log_totals)
        mixed = (
            jnp.einsum(
                "kgst,tkd->skgd",
                probs.astype(jnp.bfloat16),
                values,
                preferred_element_type=jnp.float32,
            )
            .reshape(seq_len, ATT)
            .astype(jnp.bfloat16)
        )
        hidden_one = embedded + jnp.dot(mixed, weight_out, preferred_element_type=jnp.float32)
        normed_two = rms_scale(hidden_one, gains[1]).astype(jnp.bfloat16)
        rows_all = lax.all_gather(normed_two, "hid", axis=0, tiled=True)
        gate_both = jnp.dot(rows_all, gate_up, preferred_element_type=jnp.float32)
        gate = gate_both[:, :ff_local]
        upward = gate_both[:, ff_local:]
        inner = (jax.nn.silu(gate) * upward).astype(jnp.bfloat16)
        hidden_two = hidden_one + lax.psum_scatter(
            jnp.dot(inner, weight_down, preferred_element_type=jnp.float32),
            "hid",
            scatter_dimension=0,
            tiled=True,
        )
        end_rows = step_ends[micro_batch, 0]
        picked_rows = hidden_two[end_rows]
        final = rms_scale(picked_rows, gains[2]).astype(jnp.bfloat16)
        head_all = lax.all_gather(final, "wide", axis=0, tiled=True)
        logits = jnp.einsum("rd,vd->rv", head_all, table_low, preferred_element_type=jnp.float32)
        local_max = jnp.max(logits, axis=1)
        local_total = jnp.sum(jnp.exp(logits - local_max[:, None]), axis=1)
        plus_value = jnp.sum(jnp.where((global_of == plus_token)[None, :], logits, 0.0), axis=1)
        minus_value = jnp.sum(jnp.where((global_of == minus_token)[None, :], logits, 0.0), axis=1)
        top, summed, plus_all, minus_all = combined_all(
            (local_max, local_total, plus_value, minus_value), "wide", combine_stats
        )
        log_sum = top + jnp.log(summed)
        group_labels = step_labels[micro_batch].reshape(-1)
        live = group_labels >= 0
        target_value = jnp.where(group_labels >= 1, plus_all, minus_all)
        row_loss = jnp.where(live, log_sum - target_value, 0.0)
        loss_local = loss_local + jnp.sum(
            lax.dynamic_slice_in_dim(row_loss, wide_index * slots, slots, 0)
        )
        count_local = count_local + jnp.sum(
            lax.dynamic_slice_in_dim(live.astype(jnp.float32), wide_index * slots, slots, 0)
        )
        target_global = jnp.where(group_labels >= 1, plus_token, minus_token)
        onehot = ((global_of[None, :] == target_global[:, None]) & live[:, None]).astype(
            jnp.float32
        )
        dlogits = (
            jnp.where(live[:, None], jnp.exp(logits - log_sum[:, None]), 0.0) - onehot
        ).astype(jnp.bfloat16)
        table_grad = jnp.einsum("rv,rd->vd", dlogits, head_all, preferred_element_type=jnp.float32)
        dfinal_part = jnp.dot(dlogits, table_low, preferred_element_type=jnp.float32)
        dfinal = lax.psum_scatter(dfinal_part, "wide", scatter_dimension=0, tiled=True)
        unused, pull_final = jax.vjp(rms_scale, picked_rows, gains[2])
        dpicked, dgain_three = pull_final(dfinal)
        dhidden_two = jnp.zeros((seq_len, D), jnp.float32).at[end_rows].add(dpicked)
        dmix = dhidden_two.astype(jnp.bfloat16)
        dmix_all = lax.all_gather(dmix, "hid", axis=0, tiled=True)
        dinner = jnp.einsum("rd,fd->rf", dmix_all, weight_down, preferred_element_type=jnp.float32)
        down_grad = jnp.einsum("rf,rd->fd", inner, dmix_all, preferred_element_type=jnp.float32)
        sigmoid_gate = jax.nn.sigmoid(gate)
        dgate = dinner * upward * sigmoid_gate * (1.0 + gate * (1.0 - sigmoid_gate))
        dupward = dinner * gate * sigmoid_gate
        dgate_up = jnp.concatenate([dgate, dupward], axis=1).astype(jnp.bfloat16)
        gate_grad = jnp.einsum("rd,rf->df", rows_all, dgate_up, preferred_element_type=jnp.float32)
        dnormed_two = lax.psum_scatter(
            jnp.einsum("rf,df->rd", dgate_up, gate_up, preferred_element_type=jnp.float32),
            "hid",
            scatter_dimension=0,
            tiled=True,
        )
        unused, pull_two = jax.vjp(rms_scale, hidden_one, gains[1])
        dnorm_two, dgain_two = pull_two(dnormed_two)
        dhidden_one = dhidden_two + dnorm_two
        dbranch = dhidden_one.astype(jnp.bfloat16)
        out_grad = jnp.einsum("sa,sd->ad", mixed, dbranch, preferred_element_type=jnp.float32)
        dmixed = (
            jnp.einsum("sd,ad->sa", dbranch, weight_out, preferred_element_type=jnp.float32)
            .astype(jnp.bfloat16)
            .reshape(seq_len, KV_HEADS, GROUP, HEAD)
        )
        probs_again = jnp.exp(masked_scores(queries, keys, allowed) - log_totals)
        dprobs = jnp.einsum("skgd,tkd->kgst", dmixed, values, preferred_element_type=jnp.float32)
        dvalues = jnp.einsum(
            "kgst,skgd->tkd",
            probs_again.astype(jnp.bfloat16),
            dmixed,
            preferred_element_type=jnp.float32,
        )
        dscores = (
            probs_again
            * (dprobs - jnp.sum(dprobs * probs_again, axis=-1, keepdims=True))
            * HEAD ** (-0.5)
        ).astype(jnp.bfloat16)
        dqueries = jnp.einsum(
            "kgst,tkd->skgd", dscores, keys, preferred_element_type=jnp.float32
        ).reshape(seq_len, HEADS, HEAD)
        dkeys = jnp.einsum("kgst,skgd->tkd", dscores, queries, preferred_element_type=jnp.float32)
        dqueries = rotate(dqueries, angles, -1.0).reshape(seq_len, ATT)
        dkeys = rotate(dkeys, angles, -1.0).reshape(seq_len, KV_HEADS * HEAD)
        dlinear = jnp.concatenate(
            [dqueries, dkeys, dvalues.reshape(seq_len, KV_HEADS * HEAD)], axis=1
        ).astype(jnp.bfloat16)
        bias_grad = jnp.sum(dlinear.astype(jnp.float32), axis=0)
        in_grad = jnp.einsum("sd,sc->dc", normed_one, dlinear, preferred_element_type=jnp.float32)
        dnormed_one = jnp.einsum(
            "sc,dc->sd", dlinear, weight_in, preferred_element_type=jnp.float32
        )
        unused, pull_one = jax.vjp(rms_scale, embedded, gains[0])
        dnorm_one, dgain_one = pull_one(dnormed_one)
        dembedded = (dhidden_one + dnorm_one).astype(jnp.bfloat16)
        dembed_all = lax.all_gather(dembedded, "wide", axis=0, tiled=True)
        table_grad = table_grad.at[safe_ids].add(
            jnp.where(inside[:, None], dembed_all, jnp.zeros((), jnp.bfloat16)).astype(jnp.float32)
        )
        small_grad = jnp.concatenate([dgain_one, dgain_two, dgain_three, bias_grad])
        local_grads = (table_grad, in_grad, out_grad, gate_grad, down_grad, small_grad)
        pending = add_tuples(pending, local_grads)
    table_g, in_g, out_g, gate_g, down_g, small_g = pending
    totals = (
        lax.psum_scatter(
            table_g.astype(jnp.bfloat16), "hid", scatter_dimension=0, tiled=True
        ).astype(jnp.float32),
        lax.psum_scatter(
            lax.psum_scatter(in_g.astype(jnp.bfloat16), "hid", scatter_dimension=1, tiled=True),
            "wide",
            scatter_dimension=0,
            tiled=True,
        ).astype(jnp.float32),
        lax.psum_scatter(
            lax.psum_scatter(out_g.astype(jnp.bfloat16), "hid", scatter_dimension=1, tiled=True),
            "wide",
            scatter_dimension=0,
            tiled=True,
        ).astype(jnp.float32),
        lax.psum_scatter(
            gate_g.reshape(D, 2, ff_local).astype(jnp.bfloat16),
            "wide",
            scatter_dimension=0,
            tiled=True,
        ).astype(jnp.float32),
        lax.psum_scatter(
            down_g.astype(jnp.bfloat16), "wide", scatter_dimension=1, tiled=True
        ).astype(jnp.float32),
        lax.psum_scatter(
            lax.psum_scatter(small_g.astype(jnp.bfloat16), "hid", scatter_dimension=0, tiled=True),
            "wide",
            scatter_dimension=0,
            tiled=True,
        ).astype(jnp.float32),
    )
    sum_squares = sum((jnp.sum(item * item) for item in totals))
    loss_total, count_total, squares = lax.psum(
        (loss_local, count_local, sum_squares), ("hid", "wide")
    )
    denom = jnp.maximum(count_total, 1.0)
    grad_norm = jnp.sqrt(squares) / denom
    factor = clip_limit / jnp.maximum(grad_norm, clip_limit)
    step_value = step_count.astype(jnp.float32)
    bias_one = 1.0 - beta_one**step_value
    bias_two = 1.0 - beta_two**step_value
    masters = (table, attn_in, attn_out, mlp_in, mlp_out, small_params)
    firsts = (table_first, attn_in_first, attn_out_first, mlp_in_first, mlp_out_first, small_first)
    seconds = (
        table_second,
        attn_in_second,
        attn_out_second,
        mlp_in_second,
        mlp_out_second,
        small_second,
    )
    results = [loss_total / denom, grad_norm]
    for grad_total, weight_old, first_old, second_old, step_rate in zip(
        totals, masters, firsts, seconds, rates
    ):
        clipped = grad_total / denom * factor
        first_new = beta_one * first_old + (1.0 - beta_one) * clipped
        second_new = beta_two * second_old + (1.0 - beta_two) * clipped * clipped
        update = (
            first_new / bias_one / (jnp.sqrt(second_new / bias_two) + adam_eps)
            + decay_rate * weight_old
        )
        results += [weight_old - step_rate * update, first_new, second_new]
    return (
        results[0],
        results[1],
        results[2],
        results[3],
        results[4],
        results[5],
        results[6],
        results[7],
        results[8],
        results[9],
        results[10],
        results[11],
        results[12],
        results[13],
        results[14],
        results[15],
        results[16],
        results[17],
        results[18],
        results[19],
    )


def solution(mesh):
    in_specs = (
        P(None, "hid", None),
        P(None, ("hid", "wide"), None),
        P(None, ("hid", "wide"), None),
        P(None, "hid", None),
        P(),
        P(("hid", "wide"), None),
        P("wide", "hid"),
        P("wide", "hid"),
        P("wide", None, "hid"),
        P("hid", "wide"),
        P(("hid", "wide")),
        P(("hid", "wide"), None),
        P("wide", "hid"),
        P("wide", "hid"),
        P("wide", None, "hid"),
        P("hid", "wide"),
        P(("hid", "wide")),
        P(("hid", "wide"), None),
        P("wide", "hid"),
        P("wide", "hid"),
        P("wide", None, "hid"),
        P("hid", "wide"),
        P(("hid", "wide")),
    )
    out_specs = (
        P(),
        P(),
        P(("hid", "wide"), None),
        P(("hid", "wide"), None),
        P(("hid", "wide"), None),
        P("wide", "hid"),
        P("wide", "hid"),
        P("wide", "hid"),
        P("wide", "hid"),
        P("wide", "hid"),
        P("wide", "hid"),
        P("wide", None, "hid"),
        P("wide", None, "hid"),
        P("wide", None, "hid"),
        P("hid", "wide"),
        P("hid", "wide"),
        P("hid", "wide"),
        P(("hid", "wide")),
        P(("hid", "wide")),
        P(("hid", "wide")),
    )
    return jax.shard_map(
        per_device, mesh=mesh, in_specs=in_specs, out_specs=out_specs, check_vma=False
    )
```

profile of v0, /device:TPU:0, one launch (start us, length us, event | category | flops | bytes accessed | tf_op | source)
XLA Modules:
  0.0 1716.1 jit_solution(8137108424376016763)
XLA Ops:
  19.5 203.7 %all-gather.19.cloned.1.call-done = bf16[9504,896]{1,0:T(8,128)(2,1)} async-done(((bf16[4752,896]{1,0:T(8,128)(2,1)}), bf16[9504,896]{1,0:T(8,128)(2,1)}) %all-gather.19.cloned.1.call-update) | async-done | bytes 17031184 | tf_op jit(solution)/shard_map/all_gather | solution.py:135
  223.3 18.4 %gather_fusion = bf16[2048,896]{1,0:T(8,128)(2,1)} fusion(bf16[9504,896]{1,0:T(8,128)(2,1)} %all-gather.19.cloned.1.call-done, s32[2048]{0:T(1024)S(1)} %broadcast_clamp_fusion.1), kind=kCustom, calls=%fused_computation | custom fusion | bytes 7348224 | tf_op jit(solution)/shard_map/gather | solution.py:166
  246.3 28.8 %all_gather.111 = bf16[896,576]{1,0:T(8,128)(2,1)S(1)} all-gather(bf16[56,576]{1,0:T(8,128)(2,1)S(1)} %convert_element_type.223), channel_id=1, replica_groups=mesh['hid'=2,'wide'=16] {'wide'}, dimensions={0}, use_global_device_ids=true | all-gather | bytes 1096704 | tf_op jit(solution)/shard_map/all_gather | solution.py:137
  277.5 18.5 %gather_fusion.2 = bf16[2048,896]{1,0:T(8,128)(2,1)} fusion(bf16[9504,896]{1,0:T(8,128)(2,1)} %all-gather.19.cloned.1.call-done, s32[2048]{0:T(1024)S(1)} %broadcast_clamp_fusion), kind=kCustom, calls=%fused_computation.2 | custom fusion | bytes 7348224 | tf_op jit(solution)/shard_map/gather | solution.py:166
  300.7 20.3 %all_gather.113 = bf16[896,448]{1,0:T(8,128)(2,1)S(1)} all-gather(bf16[56,448]{1,0:T(8,128)(2,1)S(1)} %convert_element_type.231), channel_id=1, replica_groups=mesh['hid'=2,'wide'=16] {'wide'}, dimensions={0}, use_global_device_ids=true | all-gather | bytes 852992 | tf_op jit(solution)/shard_map/all_gather | solution.py:143
  324.7 32.2 %all-reduce = bf16[1920]{0:T(1024)(128)(2,1)S(1)} all-reduce(bf16[1920]{0:T(1024)(128)(2,1)S(1)} %dynamic-update-slice), channel_id=1, replica_groups=mesh['hid'=2,'wide'=16] {'wide'}, use_global_device_ids=true, to_apply=%add | all-reduce | flops 1920 | bytes 7680
  379.7 32.7 %all-gather.21.cloned.1.call-done = bf16[896,1152]{0,1:T(8,128)(2,1)} async-done(((bf16[896,576]{0,1:T(8,128)(2,1)}), bf16[896,1152]{0,1:T(8,128)(2,1)}) %all-gather.21.cloned.1.call-update) | async-done | bytes 2064400 | tf_op jit(solution)/shard_map/all_gather | solution.py:136
  415.1 70.1 %reduce-scatter.22.cloned.1.call-done = bf16[128,896]{1,0:T(8,128)(2,1)} async-done(((bf16[2048,896]{1,0:T(8,128)(2,1)}), bf16[128,896]{1,0:T(8,128)(2,1)}) %reduce-scatter.22.cloned.1.call-update) | async-done | bytes 229392 | tf_op jit(solution)/shard_map/reduce_scatter | solution.py:167
  490.9 22.7 %all-gather.23.cloned.1.call-done = bf16[896,896]{0,1:T(8,128)(2,1)} async-done(((bf16[896,448]{0,1:T(8,128)(2,1)}), bf16[896,896]{0,1:T(8,128)(2,1)}) %all-gather.23.cloned.1.call-update) | async-done | bytes 1605648 | tf_op jit(solution)/shard_map/all_gather | solution.py:142
  534.5 33.2 %all-gather.27.cloned.1.call-done = bf16[2432,896]{0,1:T(8,128)(2,1)} async-done(((bf16[2432,56]{0,1:T(8,128)(2,1)}), bf16[2432,896]{0,1:T(8,128)(2,1)}) %all-gather.27.cloned.1.call-update) | async-done | bytes 4358160 | tf_op jit(solution)/shard_map/all_gather | solution.py:151
  617.0 21.6 %all-gather.10 = bf16[16,4,896]{2,1,0:T(4,128)(2,1)S(1)} all-gather(bf16[1,4,896]{2,1,0:T(4,128)(2,1)S(1)} %get-tuple-element.701), channel_id=1, replica_groups=mesh['hid'=2,'wide'=16] {'wide'}, dimensions={0}, use_global_device_ids=true | all-gather | bytes 121856 | tf_op jit(solution)/shard_map/all_gather | solution.py:215
  697.0 60.0 %all-reduce.19 = (f32[1024]{0:T(1024)}, f32[1024]{0:T(1024)}, f32[1024]{0:T(1024)}, f32[1024]{0:T(1024)}, f32[1024]{0:T(1024)}, /*index=5*/f32[1024]{0:T(1024)}, f32[1024]{0:T(1024)}, f32[1024]{0:T(1024)}) all-reduce(f32[1024]{0:T(1024)} %copy-done.110, f32[1024]{0:T(1024)} %dynamic-update-slice.2, ...), channel_id=2, replica_groups=mesh['hid'=2,'wide'=16] {'wide'}, use_global_device_ids=true, to_apply=%add.1 | all-reduce | flops 8192 | bytes 65536
  777.5 37.8 %while.42 = (s32[]{:T(128)}, f32[64]{0:T(128)}, f32[64]{0:T(128)}, f32[64]{0:T(128)}, f32[64]{0:T(128)}, /*index=5*/f32[16,64]{1,0:T(8,128)}, f32[16,64]{1,0:T(8...) while((s32[]{:T(128)}, f32[64]{0:T(128)}, f32[64]{0:T(128)}, ...), condition=%wide.region_13.14_spmd, body=%wide.region_12.13_spmd.sunk | while | flops 517 | bytes 3239 | solution.py:33
  815.4 38.5 %while.43 = (s32[]{:T(128)}, f32[64]{0:T(128)}, f32[64]{0:T(128)}, f32[64]{0:T(128)}, f32[64]{0:T(128)}, /*index=5*/f32[16,64]{1,0:T(8,128)}, f32[16,64]{1,0:T(8...) while((s32[]{:T(128)}, f32[64]{0:T(128)}, f32[64]{0:T(128)}, ...), condition=%wide.region_28.29_spmd, body=%wide.region_27.28_spmd.sunk | while | flops 517 | bytes 3239 | solution.py:33
  871.0 86.3 %all-reduce.25.cloned.1.call-done = (f32[64,896]{1,0:T(8,128)}, f32[64,896]{1,0:T(8,128)}) async-done(((f32[64,896]{1,0:T(8,128)}, f32[64,896]{1,0:T(8,128)}), (f32[64,896]{1,0:T(8,128)}, f32[64,896]{1,0:T(8,128)})) %all-reduce.25.cloned.1.call-update) | async-done | bytes 458768
  1105.8 17.8 %fusion.191 = f32[9504,896]{1,0:T(8,128)} fusion(bf16[64,896]{1,0:T(8,128)(2,1)S(1)} %copy-done.40, f32[64,9504]{1,0:T(8,128)} %get-tuple-element.733, s32[9504]{0:T(1024)S(1)} %fusion.132, f32[64]{0:T(128)S(1)} %copy-done.118, s32[64]{0:T(128)S(1)} %copy-done.122, pred[64]{0:T(512)(128)(4,1)S(1)} %copy-done.98), kind=kOutput, calls=%fused_computation.416 | convolution fusion | flops 1094252544 | bytes 36648640 | tf_op jit(solution)/shard_map/rv,rd->vd/dot_general | solution.py:242
  1126.3 25.6 %convolution_add_fusion = f32[9504,896]{1,0:T(8,128)} fusion(f32[9504,896]{1,0:T(8,128)} %fusion.191, bf16[64,896]{1,0:T(8,128)(2,1)S(1)} %reshape.1184, f32[64,9504]{1,0:T(8,128)S(1)} %get-tuple-element.735, f32[64]{0:T(128)S(1)} %copy-done.120, s32[9504]{0:T(1024)S(1)} %fusion.132, s32[64]{0:T(128)S(1)} %copy-done.124, pred[64]{0:T(512)(128)(4,1)S(1)} %copy-done.100), kind=kOutput, calls=%fused_computation.38 | convolution fusion | flops 1102768128 | bytes 70710976 | tf_op jit(solution)/shard_map/rv,rd->vd/dot_general | solution.py:242
  1190.4 32.7 %all-reduce.16 = bf16[1920]{0:T(1024)(128)(2,1)S(1)} all-reduce(bf16[1920]{0:T(1024)(128)(2,1)S(1)} %dynamic-slice.22), channel_id=26, replica_groups=mesh['hid'=2,'wide'=16] {'wide'}, use_global_device_ids=true, to_apply=%region_70.71.clone | all-reduce | flops 1920 | bytes 7680
  1231.0 45.6 %all-gather.31.cloned.1.call-done = bf16[2048,896]{1,0:T(8,128)(2,1)} async-done(((bf16[128,896]{1,0:T(8,128)(2,1)}), bf16[2048,896]{1,0:T(8,128)(2,1)}) %all-gather.31.cloned.1.call-update) | async-done | bytes 3670032 | tf_op jit(solution)/shard_map/all_gather | solution.py:303
  1280.2 59.7 %scatter_custom_fusion.2 = f32[9504,896]{1,0:T(8,128)} fusion(f32[9504,896]{1,0:T(8,128)} %convolution_add_fusion, s32[4096]{0:T(1024)S(1)} %bitcast.319, bf16[2048,896]{1,0:T(8,128)(2,1)} %broadcast_select_fusion, bf16[]{:T(256)} %constant.385, bf16[2048,896]{1,0:T(8,128)(2,1)} %broadcast_select_fusion.2), kind=kCustom, calls=%fused_computation.45 | custom fusion | flops 18350080 | bytes 41402880 | tf_op jit(solution)/shard_map/add | solution.py:83
  1357.4 198.6 %fusion = bf16[4768,896]{1,0:T(8,128)(2,1)} fusion(bf16[9504,896]{1,0:T(8,128)(2,1)} %convert_element_type.264), kind=kCustom, calls=%all-reduce-scatter | all-reduce-scatter fusion | flops 8544257 | bytes 25575936
  1560.8 36.7 %concatenate.119 = bf16[4784,896]{1,0:T(8,128)(2,1)} concatenate(bf16[16,896]{1,0:T(8,128)(2,1)S(1)} %collective-permute-done, bf16[4768,896]{1,0:T(8,128)(2,1)} %fusion), dimensions={0} | concatenate | bytes 17145856
  1614.5 40.1 %all-reduce.18 = (f32[]{:T(128)}, f32[]{:T(128)}, f32[]{:T(128)}) all-reduce(f32[]{:T(128)S(6)} %add.720, f32[]{:T(128)S(6)} %add.721, f32[]{:T(128)S(6)} %add.743), channel_id=1, replica_groups=mesh['hid'=2,'wide'=16] {'hid','wide'}, use_global_device_ids=true, to_apply=%region_30.31 | all-reduce | flops 3 | bytes 24 | tf_op jit(solution)/shard_map/psum | solution.py:344
  1664.3 40.2 %multiply_subtract_fusion = (f32[4752,896]{1,0:T(8,128)}, f32[4752,896]{1,0:T(8,128)}, f32[4752,896]{1,0:T(8,128)}) fusion(f32[4752,896]{1,0:T(8,128)} %param.32, f32[]{:T(128)S(6)} %sub.284, f32[]{:T(128)S(6)} %sub.283, f32[]{:T(128)S(6)} %div.335, f32[]{:T(128)S(6)} %max.34, bf16[4784,896]{1,0:T(8,128)(2,1)} %concatenate.119, u32[]{:S(6)} %subtract, ...), kind=kLoop, calls=%fused_computation.43 | loop fusion | flops 76640256 | bytes 110702608 | tf_op jit(solution)/shard_map/sub | solution.py:374
  (693 shorter events, 537.6 us)
Async XLA Ops:
  7.2 216.1 %all-gather.19.cloned.1.call-start = ((), (), s32[]{:S(2)}) async-start(), calls=%async_computation.10 | async-start | bytes 25546752 | tf_op jit(solution)/shard_map/all_gather | solution.py:135
  16.3 350.0 %all-gather.25.cloned.1.call-start = ((), (), s32[]{:S(2)}) async-start(), calls=%async_computation.14 | async-start | bytes 9261056 | tf_op jit(solution)/shard_map/all_gather | solution.py:148
  18.7 359.9 %reduce-scatter.18.cloned.1.call-start = ((), (), s32[]{:S(2)}) async-start(), calls=%async_computation.11 | async-start | bytes 3899392 | tf_op jit(solution)/shard_map/reduce_scatter | solution.py:167
  18.8 277.3 %copy-start.101 = (pred[2048]{0:T(1024)(128)(4,1)}, pred[2048]{0:T(1024)(128)(4,1)S(1)}, u32[]{:S(2)}) copy-start(pred[2048]{0:T(1024)(128)(4,1)S(1)} %get-tuple-element.652) | copy-start | bytes 6148
  245.4 167.0 %all-gather.21.cloned.1.call-start = ((), (), s32[]{:S(2)}) async-start(), calls=%async_computation.12 | async-start | bytes 3096576 | tf_op jit(solution)/shard_map/all_gather | solution.py:136
  276.8 208.4 %reduce-scatter.22.cloned.1.call-start = ((), (), s32[]{:S(2)}) async-start(), calls=%async_computation.17 | async-start | bytes 3899392 | tf_op jit(solution)/shard_map/reduce_scatter | solution.py:167
  299.9 213.8 %all-gather.23.cloned.1.call-start = ((), (), s32[]{:S(2)}) async-start(), calls=%async_computation.13 | async-start | bytes 2408448 | tf_op jit(solution)/shard_map/all_gather | solution.py:142
  322.2 245.5 %all-gather.27.cloned.1.call-start = ((), (), s32[]{:S(2)}) async-start(), calls=%async_computation.15 | async-start | bytes 4630528 | tf_op jit(solution)/shard_map/all_gather | solution.py:151
  323.1 276.1 %reduce-scatter.20.cloned.1.call-start = ((), (), s32[]{:S(2)}) async-start(), calls=%async_computation.16 | async-start | bytes 1376256 | tf_op jit(solution)/shard_map/reduce_scatter | solution.py:206
  361.8 254.7 %copy-start.85 = (f32[896]{0:T(1024)}, f32[896]{0:T(1024)S(1)}, u32[]{:S(2)}) copy-start(f32[896]{0:T(1024)S(1)} %get-tuple-element.684) | copy-start | bytes 10756
  365.1 231.7 %copy-start.141 = (pred[64]{0:T(512)(128)(4,1)}, pred[64]{0:T(512)(128)(4,1)S(1)}, u32[]{:S(2)}) copy-start(pred[64]{0:T(512)(128)(4,1)S(1)} %ge.81) | copy-start | bytes 196
  365.3 232.0 %copy-start.142 = (pred[64]{0:T(512)(128)(4,1)}, pred[64]{0:T(512)(128)(4,1)S(1)}, u32[]{:S(2)}) copy-start(pred[64]{0:T(512)(128)(4,1)S(1)} %ge.85) | copy-start | bytes 196
  572.5 41.7 %reduce-scatter.24.cloned.1.call-start = ((), (), s32[]{:S(2)}) async-start(), calls=%async_computation.18 | async-start | bytes 1376256 | tf_op jit(solution)/shard_map/reduce_scatter | solution.py:206
  596.1 361.1 %all-reduce.25.cloned.1.call-start = ((), (), s32[]{:S(2)}) async-start(), calls=%async_computation.27 | async-start | bytes 917504
  870.3 144.9 %reduce-scatter.28.cloned.1.call-start = ((), (), s32[]{:S(2)}) async-start(), calls=%async_computation.21 | async-start | bytes 1376256 | tf_op jit(solution)/shard_map/reduce_scatter | solution.py:257
  984.9 47.4 %reduce-scatter.26.cloned.1.call-start = ((), (), s32[]{:S(2)}) async-start(), calls=%async_computation.19 | async-start | bytes 1376256 | tf_op jit(solution)/shard_map/reduce_scatter | solution.py:257
  1015.1 67.4 %reduce-scatter.32.cloned.1.call-start = ((), (), s32[]{:S(2)}) async-start(), calls=%async_computation.24 | async-start | bytes 2408448 | tf_op jit(solution)/shard_map/reduce_scatter | solution.py:322
  1055.8 168.0 %reduce-scatter.30.cloned.1.call-start = ((), (), s32[]{:S(2)}) async-start(), calls=%async_computation.23 | async-start | bytes 3096576 | tf_op jit(solution)/shard_map/reduce_scatter | solution.py:316
  1079.8 144.0 %reduce-scatter.34.cloned.1.call-start = ((), (), s32[]{:S(2)}) async-start(), calls=%async_computation.25 | async-start | bytes 974848 | tf_op jit(solution)/shard_map/reduce_scatter | solution.py:321
  1084.7 142.7 %all-gather.29.cloned.1.call-start = ((), (), s32[]{:S(2)}) async-start(), calls=%async_computation.20 | async-start | bytes 3899392 | tf_op jit(solution)/shard_map/all_gather | solution.py:303
  1089.7 186.9 %all-gather.31.cloned.1.call-start = ((), (), s32[]{:S(2)}) async-start(), calls=%async_computation.22 | async-start | bytes 3899392 | tf_op jit(solution)/shard_map/all_gather | solution.py:303
  1090.3 468.8 %reduce-scatter.36.cloned.1.call-start = ((), (), s32[]{:S(2)}) async-start(), calls=%async_computation.26 | async-start | bytes 4630528
  1105.0 501.0 %all-reduce.27.cloned.1.call-start = ((), (), s32[]{:S(2)}) async-start(), calls=%async_computation.28 | async-start | bytes 19496960
  1556.7 4.1 collective-permute-start
  (167 other events, 3133.9 us)
Sparse Core Ops, SparseCore 0:
  16.4 206.8 all-gather.18
  226.0 80.6 all-gather.24
  311.2 67.3 reduce-scatter.17
  380.6 31.7 all-gather.20
  416.6 68.5 reduce-scatter.21
  487.2 26.4 all-gather.22
  516.4 51.3 all-gather.26
  572.6 19.8 reduce-scatter.19
  596.2 17.8 reduce-scatter.23
  870.4 86.7 all-reduce.24
  985.0 21.8 reduce-scatter.27
  1015.2 17.0 reduce-scatter.25
  1055.9 26.5 reduce-scatter.31
  1085.1 31.5 reduce-scatter.29
  1120.7 57.2 reduce-scatter.33
  1180.7 46.6 all-gather.28
  1230.1 46.4 all-gather.30
  1280.3 83.2 reduce-scatter.35
  1368.0 189.6 all-reduce.26
where the time goes:
time: 1730 us; the launch traced here: 1720 us
  waiting for transfers between devices  534 us (31%)
  blocking collectives  503 us (29%)
  other arithmetic  284 us (16%)
  matrix products  195 us (11%)
  local copies, waits for them, and re-layouts  163 us (9%)
  between operations  32.9 us (2%)
    unnamed x5, blocking collectives  328 us
    all_gather x1, waiting for transfers between devices, per_device(): lax.all_gather(table.astype(jnp.bfloat16), 'hid', axis=0, tiled=True)  204 us
    unnamed x23, waiting for transfers between devices  87.1 us
    unnamed x372, local copies, waits for them, and re-layouts  82.3 us
    reduce_scatter x2, waiting for transfers between devices, per_device(): lax.psum_scatter(picked, 'wide', scatter_dimension=0, tiled=True)  74 us
    add x1, other arithmetic, add_tuples(): return jax.tree.map(jnp.add, left, right)  59.7 us
    sub x6, other arithmetic, per_device(): results += [weight_old - step_rate * update, first_new, second_new]  49.9 us
    all_gather x2, waiting for transfers between devices, per_device(): dembed_all = lax.all_gather(dembedded, 'wide', axis=0, tiled=True)  47.7 us
  transfers between devices with their start and end apart: 20, of which 12 were waited for; matrix products, arithmetic and copies ran while one was open for 33% of the time, Pallas kernels for 0%

commit v1 on v0

v1 whole, which is shorter than its diff:
```python
import functools

import jax
import jax.numpy as jnp
from jax import lax
from jax.experimental import pallas as pl
from jax.experimental.pallas import tpu as pltpu
from jax.sharding import PartitionSpec as P

D = 896
HEADS = 14
KV_HEADS = 2
HEAD = 64
ATT = 896
GROUP = 7
KVW = KV_HEADS * HEAD

norm_eps = 1e-06
rope_base = 1000000.0
plus_token = 10
minus_token = 12
clip_limit = 0.05
beta_one = 0.9
beta_two = 0.95
adam_eps = 1e-08
decay_rate = 0.1
rates = (0.03, 0.015, 0.015, 0.015, 0.0015, 0.3)

MESH = pl.DeviceIdType.MESH
f32 = jnp.float32
bf16 = jnp.bfloat16


def exchange_kernel(hid_count, wide_count, modes, *refs):
    count = len(modes)
    ins, outs = refs[:count], refs[count : 2 * count]
    send_sems, recv_sems, local_sems = refs[2 * count :]
    h = lax.axis_index("hid")
    w = lax.axis_index("wide")
    me = h * wide_count + w
    total = hid_count * wide_count
    barrier = pltpu.get_barrier_semaphore()

    def greet(k, carry):
        other = lax.rem(me + k, total)
        pl.semaphore_signal(
            barrier, inc=1, device_id=(other // wide_count, other % wide_count), device_id_type=MESH
        )
        return carry

    lax.fori_loop(1, total, greet, 0)
    pl.semaphore_wait(barrier, total - 1)
    for i, (mode, group) in enumerate(modes):
        size = {"all": total, "wide": wide_count, "hid": hid_count}[group]
        mine = {"all": me, "wide": w, "hid": h}[group]

        def start(k, carry, i=i, mode=mode, group=group, size=size, mine=mine):
            other = lax.rem(mine + k, size)
            target = {
                "all": (other // wide_count, other % wide_count),
                "wide": (h, other),
                "hid": (other, w),
            }[group]
            pltpu.make_async_remote_copy(
                src_ref=ins[i].at[other] if mode == "a2a" else ins[i],
                dst_ref=outs[i].at[mine],
                send_sem=send_sems.at[i],
                recv_sem=recv_sems.at[i],
                device_id=target,
                device_id_type=MESH,
            ).start()
            return carry

        lax.fori_loop(1, size, start, 0)
        pltpu.make_async_copy(
            ins[i].at[mine] if mode == "a2a" else ins[i], outs[i].at[mine], local_sems.at[i]
        ).start()
    for i, (mode, group) in enumerate(modes):
        size = {"all": total, "wide": wide_count, "hid": hid_count}[group]
        mine = {"all": me, "wide": w, "hid": h}[group]
        rest = outs[i].at[pl.ds(0, size - 1)]
        pltpu.make_async_copy(
            ins[i].at[mine] if mode == "a2a" else ins[i], outs[i].at[mine], local_sems.at[i]
        ).wait()
        pltpu.make_async_copy(rest, rest, send_sems.at[i]).wait()
        pltpu.make_async_copy(rest, rest, recv_sems.at[i]).wait()


def exchange(ident, *items):
    hid_count = lax.axis_size("hid")
    wide_count = lax.axis_size("wide")
    sizes = {"all": hid_count * wide_count, "wide": wide_count, "hid": hid_count}
    modes = tuple((mode, group) for _, mode, group in items)
    shapes = [
        jax.ShapeDtypeStruct(
            item.shape if mode == "a2a" else (sizes[group],) + item.shape, item.dtype
        )
        for item, mode, group in items
    ]
    count = len(items)
    return pl.pallas_call(
        functools.partial(exchange_kernel, hid_count, wide_count, modes),
        out_shape=shapes,
        in_specs=[pl.BlockSpec(memory_space=pl.ANY)] * count,
        out_specs=[pl.BlockSpec(memory_space=pl.ANY)] * count,
        scratch_shapes=[pltpu.SemaphoreType.DMA((count,))] * 3,
        compiler_params=pltpu.CompilerParams(collective_id=ident, has_side_effects=True),
        name="exchange_%d" % ident,
    )(*[item for item, _, _ in items])


def dot(a, b, spec):
    return jnp.einsum(spec, a, b, preferred_element_type=f32)


def rms_r(rows):
    return lax.rsqrt(jnp.mean(rows * rows, axis=-1, keepdims=True) + norm_eps)


def rms_back(x, gain, dy):
    r = rms_r(x)
    dx = r * gain * dy - x * (r * r * r) * jnp.mean(x * gain * dy, axis=-1, keepdims=True)
    return dx, jnp.sum(dy * x * r, axis=0)


def rotate(values, cosine, sine):
    half = HEAD // 2
    a, b = values[..., :half], values[..., half:]
    return jnp.concatenate([a * cosine - b * sine, b * cosine + a * sine], axis=-1)


def per_device(
    token_ids,
    segment_ids,
    step_ends,
    step_labels,
    step_count,
    table,
    attn_in,
    attn_out,
    mlp_in,
    mlp_out,
    small_params,
    table_first,
    attn_in_first,
    attn_out_first,
    mlp_in_first,
    mlp_out_first,
    small_first,
    table_second,
    attn_in_second,
    attn_out_second,
    mlp_in_second,
    mlp_out_second,
    small_second,
):
    h = lax.axis_index("hid")
    w = lax.axis_index("wide")
    hid_count = lax.axis_size("hid")
    wide_count = lax.axis_size("wide")
    total = hid_count * wide_count
    me = h * wide_count + w
    micro, group_seqs, seq_len = token_ids.shape
    slots = step_ends.shape[2]
    picks = micro * slots
    tokens = micro * seq_len
    block_rows = table.shape[0]
    cap = 2 * seq_len // wide_count
    d_local = attn_in.shape[0]
    in_cols = attn_in.shape[1]
    out_cols = attn_out.shape[1]
    ff_part = mlp_in.shape[2] // wide_count
    small_local = small_params.shape[0]
    ranks = micro * cap

    ids_labels = jnp.concatenate([token_ids, step_labels], axis=2)
    ids_labels = ids_labels.reshape(micro * group_seqs, seq_len + slots)
    small_send = jnp.pad(small_params.astype(bf16).astype(f32), (0, 128 - small_local))[None]
    mlp_low = jnp.concatenate(
        [
            mlp_in.astype(bf16).reshape(d_local, 2, wide_count, ff_part).transpose(2, 0, 1, 3).reshape(
                wide_count, d_local, 2 * ff_part
            ),
            mlp_out.astype(bf16).reshape(wide_count, ff_part, d_local).transpose(0, 2, 1),
        ],
        axis=2,
    )
    il_all, small_all = exchange(0, (ids_labels, "ag", "hid"), (small_send, "ag", "all"))
    il_all = il_all.reshape(hid_count, micro, group_seqs, seq_len + slots).transpose(1, 0, 2, 3)
    il_all = il_all.reshape(micro, total, seq_len + slots)
    ids_all = il_all[:, :, :seq_len]
    labels_all = il_all[:, :, seq_len:]
    smalls = small_all[:, 0, :small_local].reshape(-1)
    gains = smalls[: 3 * D].reshape(3, D)
    bias = smalls[3 * D :]
    in_low = lax.all_gather(attn_in.astype(bf16), ("hid", "wide"))
    out_low = lax.all_gather(attn_out.astype(bf16), ("hid", "wide"))
    w_in = in_low.reshape(hid_count, D, in_cols).transpose(1, 0, 2).reshape(D, hid_count * in_cols)
    w_out = out_low.reshape(hid_count, ATT, out_cols).transpose(1, 0, 2).reshape(ATT, D)

    mine = ids_all // block_rows == me
    rank_mine = jnp.cumsum(mine.astype(jnp.int32), axis=2) - 1
    slot_iota = jnp.arange(cap, dtype=jnp.int32)
    hit = mine[:, :, None, :] & (rank_mine[:, :, None, :] == slot_iota[None, None, :, None])
    slot_row = jnp.sum(
        jnp.where(hit, (ids_all - me * block_rows)[:, :, None, :] + 1, 0), axis=3
    ) - 1
    slot_row = slot_row.transpose(1, 0, 2).reshape(total * ranks)
    send_rows = table[jnp.maximum(slot_row, 0)].astype(bf16).reshape(total, ranks, D)
    recv_rows, w_all = exchange(1, (send_rows, "a2a", "all"), (mlp_low, "a2a", "wide"))
    w_all = w_all.reshape(D, 3 * ff_part)

    own_ids = lax.dynamic_slice_in_dim(token_ids, w, 1, 1)[:, 0]
    own_block = own_ids // block_rows
    earlier = jnp.tril(jnp.ones((seq_len, seq_len), bool), -1)
    own_rank = jnp.sum(
        (own_block[:, :, None] == own_block[:, None, :]) & earlier[None], axis=2, dtype=jnp.int32
    )
    place = own_block * ranks + jnp.arange(micro, dtype=jnp.int32)[:, None] * cap + own_rank
    place = place.reshape(tokens)
    select = (place[:, None] == jnp.arange(total * ranks, dtype=jnp.int32)[None, :]).astype(bf16)
    embedded = dot(select, recv_rows.reshape(total * ranks, D), "tr,rd->td")
    segment = segment_ids[:, 0]
    ends = step_ends[:, 0]
    same = segment[:, :, None] == segment[:, None, :]
    position = jnp.sum(same & earlier[None], axis=2).astype(f32)
    frequency = rope_base ** (-jnp.arange(HEAD // 2, dtype=f32) / (HEAD // 2))
    angle = position[:, :, None] * frequency
    cosine, sine = jnp.cos(angle), jnp.sin(angle)
    cos_p = jnp.take_along_axis(cosine, ends[:, :, None], axis=1)
    sin_p = jnp.take_along_axis(sine, ends[:, :, None], axis=1)
    places = jnp.arange(seq_len, dtype=jnp.int32)
    seg_p = jnp.take_along_axis(segment, ends, axis=1)
    allowed = (seg_p[:, :, None] == segment[:, None, :]) & (places[None, None] <= ends[:, :, None])
    pick_at = (jnp.arange(micro, dtype=jnp.int32)[:, None] * seq_len + ends).reshape(picks)

    normed_one = (embedded * rms_r(embedded) * gains[0]).astype(bf16)
    emb_p = embedded[pick_at]
    n1_p = normed_one[pick_at]
    kv = dot(normed_one, w_in[:, ATT:], "td,dc->tc") + bias[ATT:]
    keys = rotate(kv[:, :KVW].reshape(micro, seq_len, KV_HEADS, HEAD), cosine[:, :, None], sine[:, :, None])
    keys = keys.astype(bf16)
    values = kv[:, KVW:].reshape(micro, seq_len, KV_HEADS, HEAD).astype(bf16)
    q = dot(n1_p, w_in[:, :ATT], "td,dc->tc") + bias[:ATT]
    queries = rotate(q.reshape(micro, slots, HEADS, HEAD), cos_p[:, :, None], sin_p[:, :, None])
    queries = queries.astype(bf16).reshape(micro, slots, KV_HEADS, GROUP, HEAD)
    scores = dot(queries, keys, "mskgd,mtkd->mkgst") * HEAD ** (-0.5)
    scores = jnp.where(allowed[:, None, None], scores, -1e30)
    probs = jax.nn.softmax(scores, axis=-1)
    probs_low = probs.astype(bf16)
    mixed = dot(probs_low, values, "mkgst,mtkd->mskgd").reshape(picks, ATT).astype(bf16)
    hidden_one = emb_p + dot(mixed, w_out, "ta,ad->td")
    n2 = (hidden_one * rms_r(hidden_one) * gains[1]).astype(bf16)

    (n2_all,) = exchange(2, (n2, "ag", "all"))
    n2_all = n2_all.reshape(total * picks, D)
    gate_up = dot(n2_all, w_all[:, : 2 * ff_part], "rd,df->rf")
    gate, upward = gate_up[:, :ff_part], gate_up[:, ff_part:]
    sig = jax.nn.sigmoid(gate)
    inner = (gate * sig * upward).astype(bf16)
    down_part = dot(inner, w_all[:, 2 * ff_part :], "rf,df->rd").astype(bf16)
    (down_recv,) = exchange(3, (down_part.reshape(total, picks, D), "a2a", "all"))
    hidden_two = hidden_one + jnp.sum(down_recv.astype(f32), axis=0)
    final = (hidden_two * rms_r(hidden_two) * gains[2]).astype(bf16)

    (final_all,) = exchange(4, (final, "ag", "all"))
    final_all = final_all.reshape(total * picks, D)
    table_low = table.astype(bf16)
    logits = dot(final_all, table_low, "rd,vd->rv")
    global_of = me * block_rows + jnp.arange(block_rows, dtype=jnp.int32)
    local_max = jnp.max(logits, axis=1)
    local_sum = jnp.sum(jnp.exp(logits - local_max[:, None]), axis=1)
    plus_value = jnp.sum(jnp.where((global_of == plus_token)[None], logits, 0.0), axis=1)
    minus_value = jnp.sum(jnp.where((global_of == minus_token)[None], logits, 0.0), axis=1)
    labels = labels_all.transpose(1, 0, 2).reshape(total * picks)
    live = labels >= 0
    target_value = jnp.where(labels >= 1, plus_value, minus_value)
    stats = jnp.stack([local_max, local_sum, target_value])
    (stats_all,) = exchange(5, (stats, "ag", "all"))
    top = jnp.max(stats_all[:, 0], axis=0)
    summed = jnp.sum(stats_all[:, 1] * jnp.exp(stats_all[:, 0] - top[None]), axis=0)
    log_sum = top + jnp.log(summed)
    loss_total = jnp.sum(jnp.where(live, log_sum - jnp.sum(stats_all[:, 2], axis=0), 0.0))
    count_total = jnp.sum(live.astype(f32))
    target_global = jnp.where(labels >= 1, plus_token, minus_token)
    onehot = ((global_of[None, :] == target_global[:, None]) & live[:, None]).astype(f32)
    dlogits = (
        jnp.where(live[:, None], jnp.exp(logits - log_sum[:, None]), 0.0) - onehot
    ).astype(bf16)
    dfinal_part = dot(dlogits, table_low, "rv,vd->rd").astype(bf16)
    (dfinal_recv,) = exchange(6, (dfinal_part.reshape(total, picks, D), "a2a", "all"))
    dfinal = jnp.sum(dfinal_recv.astype(f32), axis=0)
    dh2, dgain_three = rms_back(hidden_two, gains[2], dfinal)
    dmix = dh2.astype(bf16)

    (dmix_all,) = exchange(7, (dmix, "ag", "all"))
    dmix_all = dmix_all.reshape(total * picks, D)
    dinner = dot(dmix_all, w_all[:, 2 * ff_part :], "rd,df->rf")
    dgate = dinner * upward * sig * (1.0 + gate * (1.0 - sig))
    dupward = dinner * gate * sig
    dgu = jnp.concatenate([dgate, dupward], axis=1).astype(bf16)
    dn2_part = dot(dgu, w_all[:, : 2 * ff_part], "rf,df->rd").astype(bf16)
    mlp_grad = jnp.concatenate(
        [dot(n2_all, dgu, "rd,rf->df"), dot(dmix_all, inner, "rd,rf->df")], axis=1
    ).astype(bf16)
    dn2_recv, mlp_recv = exchange(
        8,
        (dn2_part.reshape(total, picks, D), "a2a", "all"),
        (mlp_grad.reshape(wide_count, d_local, 3 * ff_part), "a2a", "wide"),
    )
    dn2 = jnp.sum(dn2_recv.astype(f32), axis=0)
    dx, dgain_two = rms_back(hidden_one, gains[1], dn2)
    dh1 = dh2 + dx

    dbranch = dh1.astype(bf16)
    dmixed = dot(dbranch, w_out, "td,ad->ta").astype(bf16).reshape(micro, slots, KV_HEADS, GROUP, HEAD)
    dprobs = dot(dmixed, values, "mskgd,mtkd->mkgst")
    dvalues = dot(probs_low, dmixed, "mkgst,mskgd->mtkd")
    dscores = (
        probs * (dprobs - jnp.sum(dprobs * probs, axis=-1, keepdims=True)) * HEAD ** (-0.5)
    ).astype(bf16)
    dq = dot(dscores, keys, "mkgst,mtkd->mskgd").reshape(micro, slots, HEADS, HEAD)
    dk = dot(dscores, queries, "mkgst,mskgd->mtkd")
    dq = rotate(dq, cos_p[:, :, None], -sin_p[:, :, None]).reshape(picks, ATT).astype(bf16)
    dk = rotate(dk, cosine[:, :, None], -sine[:, :, None]).reshape(tokens, KVW)
    dkv = jnp.concatenate([dk, dvalues.reshape(tokens, KVW)], axis=1).astype(bf16)
    bias_grad = jnp.concatenate(
        [jnp.sum(dq.astype(f32), axis=0), jnp.sum(dkv.astype(f32), axis=0)]
    )
    kv_grad = dot(normed_one, dkv, "td,tc->dc").astype(bf16)
    pick_hot = (jnp.arange(tokens, dtype=jnp.int32)[:, None] == pick_at[None, :]).astype(f32)
    dn1_p = dot(dq, w_in[:, :ATT], "tc,dc->td")
    spread = jnp.einsum(
        "tp,pd->td",
        pick_hot,
        jnp.concatenate([dn1_p, dh1], axis=1),
        precision=lax.Precision.HIGHEST,
    )
    dn1 = dot(dkv, w_in[:, ATT:], "tc,dc->td") + spread[:, :D]
    dx, dgain_one = rms_back(embedded, gains[0], dn1)
    dembedded = (spread[:, D:] + dx).astype(bf16)

    demb_send = dot(select, dembedded, "tr,td->rd").astype(bf16).reshape(total, ranks, D)
    dq_wide = jnp.pad(dq, ((0, 0), (0, 2 * KVW))).reshape(picks, hid_count, 1, in_cols)
    db_wide = dbranch.reshape(picks, hid_count, 1, out_cols)

    def spread_to(rows, dims):
        return jnp.broadcast_to(rows, (picks, hid_count, wide_count, dims))

    grads_send = jnp.concatenate(
        [
            spread_to(dq_wide, in_cols),
            spread_to(db_wide, out_cols),
            spread_to(n1_p.reshape(picks, 1, wide_count, d_local), d_local),
            spread_to(mixed.reshape(picks, 1, wide_count, d_local), d_local),
        ],
        axis=3,
    )
    grads_send = grads_send.transpose(1, 2, 0, 3).reshape(total, picks, -1)
    small_grad = jnp.concatenate([dgain_one, dgain_two, dgain_three, bias_grad])
    small_grad = jnp.pad(small_grad.reshape(total, 1, small_local), ((0, 0), (0, 0), (0, 128 - small_local)))
    demb_recv, rows_recv, kv_recv, small_recv = exchange(
        9,
        (demb_send, "a2a", "all"),
        (grads_send, "a2a", "all"),
        (kv_grad.reshape(wide_count, d_local, 2 * KVW), "a2a", "wide"),
        (small_grad, "a2a", "all"),
    )
    rows_recv = rows_recv.reshape(total * picks, -1)
    c0, c1, c2 = in_cols, in_cols + out_cols, in_cols + out_cols + d_local
    in_g = dot(rows_recv[:, c1:c2], rows_recv[:, :c0], "rd,rc->dc")
    out_g = dot(rows_recv[:, c2:], rows_recv[:, c0:c1], "ra,rd->ad")
    kv_sum = jnp.sum(kv_recv.astype(f32), axis=0)
    table_g = dot(dlogits, final_all, "rv,rd->vd") + dot(
        (slot_row[:, None] == jnp.arange(block_rows, dtype=jnp.int32)[None, :]).astype(bf16),
        demb_recv.reshape(total * ranks, D),
        "rv,rd->vd",
    )
    (kv_all,) = exchange(10, (kv_sum, "ag", "hid"))
    kv_full = jnp.pad(jnp.sum(kv_all, axis=0), ((0, 0), (ATT, 0)))
    in_g = in_g + lax.dynamic_slice_in_dim(kv_full, h * in_cols, in_cols, 1)
    mlp_g = mlp_recv.astype(f32)
    gate_g = (
        mlp_g[:, :, : 2 * ff_part]
        .reshape(wide_count, d_local, 2, ff_part)
        .transpose(1, 2, 0, 3)
        .reshape(d_local, 2, wide_count * ff_part)
    )
    down_g = mlp_g[:, :, 2 * ff_part :].transpose(0, 2, 1).reshape(wide_count * ff_part, d_local)
    small_g = jnp.sum(small_recv[:, 0, :small_local], axis=0)
    totals = (table_g, in_g, out_g, gate_g, down_g, small_g)
    sum_squares = sum((jnp.sum(item * item) for item in totals))
    (squares_all,) = exchange(11, (jnp.full((1, 128), sum_squares), "ag", "all"))
    squares = jnp.sum(squares_all[:, 0, 0])

    denom = jnp.maximum(count_total, 1.0)
    grad_norm = jnp.sqrt(squares) / denom
    factor = clip_limit / jnp.maximum(grad_norm, clip_limit)
    step_value = step_count.astype(f32)
    bias_one = 1.0 - beta_one**step_value
    bias_two = 1.0 - beta_two**step_value
    masters = (table, attn_in, attn_out, mlp_in, mlp_out, small_params)
    firsts = (table_first, attn_in_first, attn_out_first, mlp_in_first, mlp_out_first, small_first)
    seconds = (
        table_second,
        attn_in_second,
        attn_out_second,
        mlp_in_second,
        mlp_out_second,
        small_second,
    )
    results = [loss_total / denom, grad_norm]
    for grad_total, weight_old, first_old, second_old, step_rate in zip(
        totals, masters, firsts, seconds, rates
    ):
        clipped = grad_total / denom * factor
        first_new = beta_one * first_old + (1.0 - beta_one) * clipped
        second_new = beta_two * second_old + (1.0 - beta_two) * clipped * clipped
        update = (
            first_new / bias_one / (jnp.sqrt(second_new / bias_two) + adam_eps)
            + decay_rate * weight_old
        )
        results += [weight_old - step_rate * update, first_new, second_new]
    return tuple(results)


def solution(mesh):
    in_specs = (
        P(None, "hid", None),
        P(None, ("hid", "wide"), None),
        P(None, ("hid", "wide"), None),
        P(None, "hid", None),
        P(),
        P(("hid", "wide"), None),
        P("wide", "hid"),
        P("wide", "hid"),
        P("wide", None, "hid"),
        P("hid", "wide"),
        P(("hid", "wide")),
        P(("hid", "wide"), None),
        P("wide", "hid"),
        P("wide", "hid"),
        P("wide", None, "hid"),
        P("hid", "wide"),
        P(("hid", "wide")),
        P(("hid", "wide"), None),
        P("wide", "hid"),
        P("wide", "hid"),
        P("wide", None, "hid"),
        P("hid", "wide"),
        P(("hid", "wide")),
    )
    out_specs = (
        P(),
        P(),
        P(("hid", "wide"), None),
        P(("hid", "wide"), None),
        P(("hid", "wide"), None),
        P("wide", "hid"),
        P("wide", "hid"),
        P("wide", "hid"),
        P("wide", "hid"),
        P("wide", "hid"),
        P("wide", "hid"),
        P("wide", None, "hid"),
        P("wide", None, "hid"),
        P("wide", None, "hid"),
        P("hid", "wide"),
        P("hid", "wide"),
        P("hid", "wide"),
        P(("hid", "wide")),
        P(("hid", "wide")),
        P(("hid", "wide")),
    )
    return jax.shard_map(
        per_device, mesh=mesh, in_specs=in_specs, out_specs=out_specs, check_vma=False
    )
```

time: 1730 us -> 573 us (0.33)
  waiting for transfers between devices: 534 us -> 15.8 us
  blocking collectives: 503 us -> 0 us
  Pallas kernels: 0 us -> 280 us
  other arithmetic: 284 us -> 93.7 us
  matrix products: 195 us -> 83.6 us
  local copies, waits for them, and re-layouts: 163 us -> 64.2 us
    unnamed x5 -> x0, blocking collectives: 328 us -> none
    all_gather x7 -> x2, waiting for transfers between devices: 340 us -> 15.8 us  [the longest x1 15.8 us: per_device(): in_low = lax.all_gather(attn_in.astype(bf16), ('hid', 'wide'))]
    pallas_call x0 -> x12, Pallas kernels: none -> 280 us  [exchange(): pl.pallas_call(functools.partial(exchange_kernel, hid_count, wide_count,...]
    add x67 -> x5, other arithmetic: 141 us -> 0.6 us  [the longest x1 0.51 us: per_device(): jnp.arange(micro, dtype=jnp.int32)[:, None] * seq_len + ends]
    all_gather x9 -> x0, blocking collectives: 135 us -> none  [the longest x2 39.4 us: per_device(): head_all = lax.all_gather(final, 'wide', axis=0, tiled=True)]
    dot_general x42 -> x27, matrix products: 195 us -> 82 us  [the longest x26 81.1 us: dot(): return jnp.einsum(spec, a, b, preferred_element_type=f32)]
    reduce_scatter x9 -> x0, waiting for transfers between devices: 107 us -> none  [the longest x2 74 us: per_device(): lax.psum_scatter(picked, 'wide', scatter_dimension=0, tiled=True)]
    unnamed x23 -> x2, waiting for transfers between devices: 87.1 us -> 0.03 us
  transfers between devices with their start and end apart: 20 -> 2, of which waited for: 12 -> 1; matrix products, arithmetic and copies ran while one was open for 33% -> 9% of each run, Pallas kernels for 0% -> 13%
where the time goes in v1:
time: 573 us; the launch traced here: 562 us
  Pallas kernels  280 us (49%)
  other arithmetic  93.7 us (16%)
  matrix products  83.6 us (15%)
  local copies, waits for them, and re-layouts  64.2 us (11%)
  between operations  24.8 us (4%)
  waiting for transfers between devices  15.8 us (3%)
    pallas_call x12, Pallas kernels, exchange(): pl.pallas_call(functools.partial(exchange_kernel, hid_count, wide_count,...  280 us
    dot_general x26, matrix products, dot(): return jnp.einsum(spec, a, b, preferred_element_type=f32)  81.1 us
    sub x6, other arithmetic, per_device(): results += [weight_old - step_rate * update, first_new, second_new]  51 us
    all_gather x1, waiting for transfers between devices, per_device(): in_low = lax.all_gather(attn_in.astype(bf16), ('hid', 'wide'))  15.8 us
    gather x1, local copies, waits for them, and re-layouts, per_device(): table[jnp.maximum(slot_row, 0)].astype(bf16).reshape(total, ranks, D)  11.6 us
  transfers between devices with their start and end apart: 2, of which 1 were waited for; matrix products, arithmetic and copies ran while one was open for 9% of the time, Pallas kernels for 13%

profile of v1, /device:TPU:0, one launch (start us, length us, event | category | flops | bytes accessed | tf_op | source)
XLA Modules:
  0.0 561.9 jit_solution(1756521761069711827)
XLA Ops:
  14.5 10.2 %exchange_0.1 = (s32[2,32,132]{2,1,0:T(8,128)}, f32[32,1,128]{2,1,0:T(1,128)}) custom-call(s32[32,132]{1,0:T(8,128)} %bitcast.267, f32[1,128]{1,0:T(1,128)} %bitcast_convert_fusion.refs_1_), custom_call_target="tpu_custom_call" | custom-call | tf_op jit(solution)/shard_map/exchange_0/pallas_call | solution.py:101
  40.7 11.6 %gather_fusion = bf16[1024,896]{1,0:T(8,128)(2,1)} fusion(f32[4752,896]{1,0:T(8,128)} %param.30, s32[1024]{0:T(1024)S(1)} %broadcast_clamp_fusion), kind=kCustom, calls=%fused_computation.2 | custom fusion | bytes 3674112 | tf_op jit(solution)/shard_map/gather | solution.py:209
  53.5 63.1 %exchange_1.1 = (bf16[32,32,896]{2,1,0:T(8,128)(2,1)}, bf16[16,56,456]{2,1,0:T(8,128)(2,1)}) custom-call(bf16[32,32,896]{2,1,0:T(8,128)(2,1)} %bitcast.238, bf16[16,56,456]{2,1,0:T(8,128)(2,1)} %pad_maximum_fusion.refs_1_), custom_call_target="tpu_custom_call" | custom-call | tf_op jit(solution)/shard_map/exchange_1/pallas_call | solution.py:101
  129.9 5.0 copy.246
  136.3 15.8 %all-gather.5.cloned.1.call-done = bf16[1792,576]{1,0:T(8,128)(2,1)} async-done(((bf16[56,576]{1,0:T(8,128)(2,1)}), bf16[1792,576]{1,0:T(8,128)(2,1)}) %all-gather.5.cloned.1.call-update) | async-done | bytes 2064400 | tf_op jit(solution)/shard_map/all_gather | solution.py:196
  152.1 5.8 %copy.243 = bf16[2,896,576]{1,0,2:T(2,128)(2,1)} copy(bf16[2,896,576]{2,1,0:T(8,128)(2,1)} %bitcast.245) | data formatting | bytes 4128768 | tf_op jit(solution)/shard_map/reshape | solution.py:198
  175.0 14.6 %exchange_2.1 = bf16[32,8,896]{2,1,0:T(8,128)(2,1)} custom-call(bf16[8,896]{1,0:T(8,128)(2,1)} %multiply_convert_fusion.5.refs_0_), custom_call_target="tpu_custom_call" | custom-call | tf_op jit(solution)/shard_map/exchange_2/pallas_call | solution.py:101
  192.4 15.0 %exchange_3.1 = bf16[32,8,896]{2,1,0:T(8,128)(2,1)} custom-call(bf16[32,8,896]{2,1,0:T(8,128)(2,1)} %fusion.16.refs_0_), custom_call_target="tpu_custom_call" | custom-call | tf_op jit(solution)/shard_map/exchange_3/pallas_call | solution.py:101
  209.3 15.2 %exchange_4.1 = bf16[32,8,896]{2,1,0:T(8,128)(2,1)} custom-call(bf16[8,896]{1,0:T(8,128)(2,1)} %multiply_convert_fusion.4.refs_0_), custom_call_target="tpu_custom_call" | custom-call | tf_op jit(solution)/shard_map/exchange_4/pallas_call | solution.py:101
  224.5 7.5 %fusion.135 = (f32[256]{0:T(256)S(1)}, f32[256,4752]{0,1:T(8,128)S(1)}) fusion(f32[4752,896]{1,0:T(8,128)} %param.30, bf16[32,8,896]{2,1,0:T(8,128)(2,1)} %exchange_4.1), kind=kOutput, calls=%fused_computation.294 | convolution fusion | flops 2185463552 | bytes 22356992 | tf_op jit(solution)/shard_map/rd,vd->rv/dot_general | solution.py:113
  235.9 10.4 %exchange_5.1 = f32[32,3,256]{2,1,0:T(4,128)} custom-call(f32[3,256]{1,0:T(4,128)} %pad_maximum_fusion.11.refs_0_), custom_call_target="tpu_custom_call" | custom-call | tf_op jit(solution)/shard_map/exchange_5/pallas_call | solution.py:101
  248.4 10.2 %fusion.18.refs_0_ = bf16[32,8,896]{2,1,0:T(8,128)(2,1)} fusion(f32[4752,896]{1,0:T(8,128)} %param.30, f32[256,4752]{0,1:T(8,128)} %copy-done.1, s32[256]{0:T(256)S(1)} %copy-done.44, f32[256]{0:T(256)S(1)} %get-tuple-element.84, s32[4752]{0:T(1024)S(1)} %iota_add_fusion, pred[256]{0:T(512)(128)(4,1)S(1)} %ge.74), kind=kOutput, calls=%fused_computation.43 | convolution fusion | flops 2192992256 | bytes 22377280 | tf_op jit(solution)/shard_map/rv,vd->rd/dot_general | solution.py:113
  258.6 15.2 %exchange_6.1 = bf16[32,8,896]{2,1,0:T(8,128)(2,1)} custom-call(bf16[32,8,896]{2,1,0:T(8,128)(2,1)} %fusion.18.refs_0_), custom_call_target="tpu_custom_call" | custom-call | tf_op jit(solution)/shard_map/exchange_6/pallas_call | solution.py:101
  276.3 15.2 %exchange_7.1 = bf16[32,8,896]{2,1,0:T(8,128)(2,1)} custom-call(bf16[8,896]{1,0:T(8,128)(2,1)} %fusion.119.refs_0_), custom_call_target="tpu_custom_call" | custom-call | tf_op jit(solution)/shard_map/exchange_7/pallas_call | solution.py:101
  300.3 29.3 %exchange_8.1 = (bf16[32,8,896]{2,1,0:T(8,128)(2,1)}, bf16[16,56,456]{2,1,0:T(8,128)(2,1)}) custom-call(bf16[32,8,896]{2,1,0:T(8,128)(2,1)} %fusion.17.refs_0_, bf16[16,56,456]{2,1,0:T(8,128)(2,1)} %pad_maximum_fusion.1.refs_1_), custom_call_target="tpu_custom_call" | custom-call | tf_op jit(solution)/shard_map/exchange_8/pallas_call | solution.py:101
  350.9 3.7 convolution_convert_fusion
  355.8 76.0 %exchange_9.1 = (bf16[32,32,896]{2,1,0:T(8,128)(2,1)}, bf16[32,8,1136]{2,1,0:T(8,128)(2,1)}, bf16[16,56,256]{2,1,0:T(8,128)(2,1)}, f32[32,1,128]{2,1,0:T(1,128)}) custom-call(bf16[32,32,896]{2,1,0:T(8,128)(2,1)} %bitcast.240, bf16[32,8,1136]{2,1,0:T(8,128)(2,1)} %bitcast.244, bf16[16,56,256]{2,1,0:T(8,128)(2,1)} %bitcast.251, f32[32,1,128]{2,1,0:T(1,128)} %pad.19.refs_3_), custom_call_target="tpu_custom_call" | custom-call | tf_op jit(solution)/shard_map/exchange_9/pallas_call | solution.py:101
  431.9 15.5 %fusion.2 = f32[4752,896]{1,0:T(8,128)} fusion(bf16[1024,896]{1,0:T(8,128)(2,1)} %bitcast.287, s32[1024]{0:T(1024)S(1)} %copy-done.65), kind=kOutput, calls=%fused_computation.10 | convolution fusion | flops 8724824064 | bytes 18870272 | tf_op jit(solution)/shard_map/rv,rd->vd/dot_general | solution.py:113
  447.4 15.3 %multiply_reduce_fusion = (f32[]{:T(128)}, f32[4752,896]{1,0:T(8,128)}) fusion(f32[4752,896]{1,0:T(8,128)} %fusion.2, bf16[32,8,896]{2,1,0:T(8,128)(2,1)S(1)} %copy-done.8, f32[256,4752]{0,1:T(8,128)S(1)} %bitcast.230, s32[256]{0:T(256)S(1)} %copy-done.45, f32[256]{0:T(256)S(1)} %copy-done.49, s32[4752]{0:T(1024)S(1)} %iota_add_fusion, ...), kind=kOutput, calls=%fused_computation.15 | convolution fusion | flops 2201278464 | bytes 39408452 | tf_op jit(solution)/shard_map/rv,rd->vd/dot_general | solution.py:113
  463.4 7.6 %exchange_10.1 = f32[2,56,256]{2,1,0:T(8,128)} custom-call(f32[56,256]{1,0:T(8,128)} %convert_reduce_fusion.refs_0_), custom_call_target="tpu_custom_call" | custom-call | tf_op jit(solution)/shard_map/exchange_10/pallas_call | solution.py:101
  479.4 8.0 %exchange_11.1 = f32[32,1,128]{2,1,0:T(1,128)} custom-call(f32[1,128]{1,0:T(1,128)} %broadcast_in_dim.179.refs_0_), custom_call_target="tpu_custom_call" | custom-call | tf_op jit(solution)/shard_map/exchange_11/pallas_call | solution.py:101
  497.1 3.5 mul.877
  502.0 42.4 %multiply_subtract_fusion = (f32[4752,896]{1,0:T(8,128)}, f32[4752,896]{1,0:T(8,128)}, f32[4752,896]{1,0:T(8,128)}) fusion(f32[4752,896]{1,0:T(8,128)} %param.30, f32[]{:T(128)S(6)} %sub.161, f32[]{:T(128)S(6)} %sub.160, f32[]{:T(128)S(6)} %div.212, f32[4752,896]{1,0:T(8,128)} %get-tuple-element.129, f32[]{:T(128)S(6)} %max.23, f32[4752,896]{1,0:T(8,128)} %param.42, ...), kind=kLoop, calls=%fused_computation.12 | loop fusion | flops 72382464 | bytes 119218192 | tf_op jit(solution)/shard_map/sub | solution.py:423
  546.1 5.1 multiply_subtract_fusion.1
  (364 shorter events, 116.0 us)
Async XLA Ops:
  7.2 122.7 %all-gather.7.cloned.1.call-start = ((), (), s32[]{:S(2)}) async-start(), calls=%async_computation.1 | async-start | bytes 1892352 | tf_op jit(solution)/shard_map/all_gather | solution.py:197
  8.9 143.2 %all-gather.5.cloned.1.call-start = ((), (), s32[]{:S(2)}) async-start(), calls=%async_computation | async-start | bytes 2365440 | tf_op jit(solution)/shard_map/all_gather | solution.py:196
  174.3 33.0 %copy-start.60 = (f32[8]{0:T(128)}, f32[8]{0:T(128)S(1)}, u32[]{:S(2)}) copy-start(f32[8]{0:T(128)S(1)} %get-tuple-element.115) | copy-start | bytes 100
  208.6 67.1 %copy-start.56 = (f32[8]{0:T(128)}, f32[8]{0:T(128)S(1)}, u32[]{:S(2)}) copy-start(f32[8]{0:T(128)S(1)} %get-tuple-element.117) | copy-start | bytes 100
  208.6 67.0 %copy-start.67 = (f32[8]{0:T(128)}, f32[8]{0:T(128)S(1)}, u32[]{:S(2)}) copy-start(f32[8]{0:T(128)S(1)} %get-tuple-element.116) | copy-start | bytes 100
  299.1 31.6 %copy-start.61 = (f32[8]{0:T(128)S(1)}, f32[8]{0:T(128)}, u32[]{:S(2)}) copy-start(f32[8]{0:T(128)} %copy-done.60) | copy-start | bytes 100
  299.1 32.4 %copy-start.57 = (f32[8]{0:T(128)S(1)}, f32[8]{0:T(128)}, u32[]{:S(2)}) copy-start(f32[8]{0:T(128)} %copy-done.56) | copy-start | bytes 100
  299.1 32.4 %copy-start.68 = (f32[8]{0:T(128)S(1)}, f32[8]{0:T(128)}, u32[]{:S(2)}) copy-start(f32[8]{0:T(128)} %copy-done.67) | copy-start | bytes 100
  299.1 33.7 %copy-start.3 = (bf16[896,2,448]{0,2,1:T(8,128)(2,1)S(1)}, bf16[896,2,448]{0,2,1:T(8,128)(2,1)}, u32[]{:S(2)}) copy-start(bf16[896,2,448]{0,2,1:T(8,128)(2,1)} %copy.214) | copy-start | bytes 4816900
  300.3 33.0 %copy-start.26 = (bf16[2,128,2,64]{1,0,3,2:T(2,128)(2,1)S(1)}, bf16[2,128,2,64]{1,0,3,2:T(2,128)(2,1)}, u32[]{:S(2)}) copy-start(bf16[2,128,2,64]{1,0,3,2:T(2,128)(2,1)} %convert_element_type.177) | copy-start | bytes 196612
  300.3 33.1 %copy-start.39 = (bf16[2,128,2,32]{1,3,2,0:T(8,128)(2,1)S(1)}, bf16[2,128,2,32]{1,3,2,0:T(8,128)(2,1)}, u32[]{:S(2)}) copy-start(bf16[2,128,2,32]{1,3,2,0:T(8,128)(2,1)} %copy-done.38) | copy-start | bytes 98308
  300.3 33.1 %copy-start.41 = (bf16[2,128,2,32]{1,3,2,0:T(8,128)(2,1)S(1)}, bf16[2,128,2,32]{1,3,2,0:T(8,128)(2,1)}, u32[]{:S(2)}) copy-start(bf16[2,128,2,32]{1,3,2,0:T(8,128)(2,1)} %copy-done.40) | copy-start | bytes 98308
  300.3 33.1 %copy-start.75 = (f32[2,2,7,4]{2,3,1,0:T(4,128)S(1)}, f32[2,2,7,4]{2,3,1,0:T(4,128)}, u32[]{:S(2)}) copy-start(f32[2,2,7,4]{2,3,1,0:T(4,128)} %copy-done.74) | copy-start | bytes 1348
  354.7 77.1 %copy-start.65 = (s32[1024]{0:T(1024)S(1)}, s32[1024]{0:T(1024)}, u32[]{:S(2)}) copy-start(s32[1024]{0:T(1024)} %eq.163) | copy-start | bytes 12292
  355.8 91.6 %slice-start = ((s8[4866048]{0:T(1024)(128)(4,1)}), s8[671744]{0:T(1024)(128)(4,1)S(1)}, s32[]{:S(2)}) async-start(s8[4866048]{0:T(1024)(128)(4,1)} %bitcast.229), calls=%async_computation.2 | async-start | bytes 1343488
  501.9 42.5 %copy-start.19 = (f32[56,576]{1,0:T(8,128)S(1)}, f32[56,576]{1,0:T(8,128)}, u32[]{:S(2)}) copy-start(f32[56,576]{1,0:T(8,128)} %param.31) | copy-start | bytes 387076
  501.9 42.5 %copy-start.20 = (f32[56,576]{1,0:T(8,128)S(1)}, f32[56,576]{1,0:T(8,128)}, u32[]{:S(2)}) copy-start(f32[56,576]{1,0:T(8,128)} %get-tuple-element.131) | copy-start | bytes 387076
  501.9 42.5 %copy-start.27 = (f32[56,576]{1,0:T(8,128)S(1)}, f32[56,576]{1,0:T(8,128)}, u32[]{:S(2)}) copy-start(f32[56,576]{1,0:T(8,128)} %param.43) | copy-start | bytes 387076
  501.9 42.5 %copy-start.28 = (f32[56,576]{1,0:T(8,128)S(1)}, f32[56,576]{1,0:T(8,128)}, u32[]{:S(2)}) copy-start(f32[56,576]{1,0:T(8,128)} %param.37) | copy-start | bytes 387076
  502.0 43.3 %copy-start.23 = (f32[56,448]{1,0:T(8,128)S(1)}, f32[56,448]{1,0:T(8,128)}, u32[]{:S(2)}) copy-start(f32[56,448]{1,0:T(8,128)} %param.32) | copy-start | bytes 301060
  502.0 43.3 %copy-start.33 = (f32[56,448]{1,0:T(8,128)S(1)}, f32[56,448]{1,0:T(8,128)}, u32[]{:S(2)}) copy-start(f32[56,448]{1,0:T(8,128)} %param.44) | copy-start | bytes 301060
  502.0 43.3 %copy-start.34 = (f32[56,448]{1,0:T(8,128)S(1)}, f32[56,448]{1,0:T(8,128)}, u32[]{:S(2)}) copy-start(f32[56,448]{1,0:T(8,128)} %param.38) | copy-start | bytes 301060
  502.0 44.1 %copy-start.16 = (f32[56,2,2432]{2,1,0:T(2,128)S(1)}, f32[56,2,2432]{2,1,0:T(2,128)}, u32[]{:S(2)}) copy-start(f32[56,2,2432]{2,1,0:T(2,128)} %param.45) | copy-start | bytes 3268612
  502.0 44.1 %copy-start.17 = (f32[56,2,2432]{2,1,0:T(2,128)S(1)}, f32[56,2,2432]{2,1,0:T(2,128)}, u32[]{:S(2)}) copy-start(f32[56,2,2432]{2,1,0:T(2,128)} %param.39) | copy-start | bytes 3268612
  (56 other events, 473.3 us)
Sparse Core Ops, SparseCore 0:
  11.5 68.7 all-gather.6
  83.8 68.2 all-gather.4
